TPU v7x, 32 devices: a whole 2x2x4 slice. The times are simulated.
32 devices in a mesh: groups: 2 (over x), gx: 8 (over z, y), gy: 2 (over core).
Axes of the slice: x: 2, y: 2, z: 4, core: 2. Of those that a mesh axis runs over, the one named last changes fastest.
Arguments:
- source: float32 [2, 3, 2, 32, 64, 256], P('groups', None, None, 'gx', 'gy'), parts along dimension 0, may hold values from -12 to 12
- permittivity: float32 [6, 32, 64, 256], P('groups', 'gx', 'gy'), parts along dimension 0, may hold values from 1 to 12
- frequency: float32 [1], replicated, may hold values from 0.25 to 0.6
Outputs:
- solution: float32 [2, 3, 2, 32, 64, 256], P('groups', None, None, 'gx', 'gy'), parts along dimension 0
- residual: float32 [2, 3, 2, 32, 64, 256], P('groups', None, None, 'gx', 'gy'), parts along dimension 0
There are 2 independent parts, one for each index of `groups`. A program takes and returns all parts, laid end to end along the dimension named above; an argument that names none is the same for every part. Nothing has to cross between parts.
All inputs are finite; a program needn't handle non-finite values.
Results may differ from a plain program's by a relative error of at most 0.0003.
Values sent between devices are 32-bit elements; how exact they have to be, the bound alone decides.
A program may use at most 64 MiB of HBM per device.

v0:
```python
import jax
import jax.numpy as jnp
from jax import lax
from jax.sharding import PartitionSpec as P

NZ = 256
PML = 8
ITERS = 3


pml_strength = 2.0


def shifted(array, axis, by):
    devices = lax.axis_size(axis)
    pairs = [(i, i + by) for i in range(devices) if 0 <= i + by < devices]
    return lax.ppermute(array, axis, pairs)


def stretch(points, length, frequency):
    inside = jnp.maximum(jnp.maximum(PML - points, points - (length - PML)), 0.0) / PML
    damping = pml_strength * inside**3 / frequency[:, None]
    factor = 1.0 / (1.0 + damping * damping)
    return jnp.stack([factor, -damping * factor], axis=1)


def orient(coefficient, dimension):
    target = [coefficient.shape[0], 2, 1, 1, 1]
    target[dimension] = coefficient.shape[2]
    return coefficient.reshape(target)


def times_coef(values, coefficient):
    real_part = values[:, 0] * coefficient[:, 0] - values[:, 1] * coefficient[:, 1]
    imag_part = values[:, 0] * coefficient[:, 1] + values[:, 1] * coefficient[:, 0]
    return jnp.stack([real_part, imag_part], axis=1)


def curl_forward(extended, front_x, front_y, front_z):
    centre = extended[:, :, :, :-1, :-1]

    def step_x(component):
        return extended[:, component, :, 1:, :-1] - centre[:, component]

    def step_y(component):
        return extended[:, component, :, :-1, 1:] - centre[:, component]

    def step_z(component):
        cells = centre[:, component]
        above = jnp.concatenate([cells[..., 1:], jnp.zeros_like(cells[..., :1])], axis=-1)
        return above - cells

    curl_x = times_coef(step_y(2), front_y) - times_coef(step_z(1), front_z)
    curl_y = times_coef(step_z(0), front_z) - times_coef(step_x(2), front_x)
    curl_z = times_coef(step_x(1), front_x) - times_coef(step_y(0), front_y)
    return jnp.stack([curl_x, curl_y, curl_z], axis=1)


def curl_backward(padded, back_x, back_y, back_z):
    centre = padded[:, :, :, 1:, 1:]

    def step_x(component):
        return centre[:, component] - padded[:, component, :, :-1, 1:]

    def step_y(component):
        return centre[:, component] - padded[:, component, :, 1:, :-1]

    def step_z(component):
        cells = centre[:, component]
        below = jnp.concatenate([jnp.zeros_like(cells[..., :1]), cells[..., :-1]], axis=-1)
        return cells - below

    out_x = times_coef(step_y(2), back_y) - times_coef(step_z(1), back_z)
    out_y = times_coef(step_z(0), back_z) - times_coef(step_x(2), back_x)
    out_z = times_coef(step_x(1), back_x) - times_coef(step_y(0), back_y)
    return jnp.stack([out_x, out_y, out_z], axis=1)


def scaled(values, number):
    real_scale = number[0].reshape(-1, 1, 1, 1, 1)
    imag_scale = number[1].reshape(-1, 1, 1, 1, 1)
    real_part = values[:, :, 0] * real_scale - values[:, :, 1] * imag_scale
    imag_part = values[:, :, 0] * imag_scale + values[:, :, 1] * real_scale
    return jnp.stack([real_part, imag_part], axis=2)


def product(left, right):
    real_part = jnp.sum(
        left[:, :, 0] * right[:, :, 0] + left[:, :, 1] * right[:, :, 1], axis=(1, 2, 3, 4)
    )
    imag_part = jnp.sum(
        left[:, :, 0] * right[:, :, 1] - left[:, :, 1] * right[:, :, 0], axis=(1, 2, 3, 4)
    )
    return jnp.stack([real_part, imag_part])


def complex_times(first, other):
    return jnp.stack(
        [first[0] * other[0] - first[1] * other[1], first[0] * other[1] + first[1] * other[0]]
    )


def complex_ratio(first, other):
    modulus = other[0] * other[0] + other[1] * other[1]
    return (
        jnp.stack(
            [first[0] * other[0] + first[1] * other[1], first[1] * other[0] - first[0] * other[1]]
        )
        / modulus
    )


def grid_points(start, first, count):
    return (start + jnp.arange(first, count, dtype=jnp.int32)).astype(jnp.float32)


def body(source, permittivity, frequency):
    cells_x = source.shape[3]
    cells_y = source.shape[4]
    total_x = cells_x * lax.axis_size("gx")
    total_y = cells_y * lax.axis_size("gy")
    index_x = lax.axis_index("gx")
    index_y = lax.axis_index("gy")
    margin = 0
    front_x = orient(
        stretch(grid_points(index_x * cells_x, -margin, cells_x) + 0.5, total_x, frequency), 2
    )
    front_y = orient(
        stretch(grid_points(index_y * cells_y, -margin, cells_y) + 0.5, total_y, frequency), 3
    )
    back_x = orient(stretch(grid_points(index_x * cells_x, 0, cells_x), total_x, frequency), 2)
    back_y = orient(stretch(grid_points(index_y * cells_y, 0, cells_y), total_y, frequency), 3)
    z_points = grid_points(0, 0, NZ)
    front_z = orient(stretch(z_points + 0.5, NZ, frequency), 4)
    back_z = orient(stretch(z_points, NZ, frequency), 4)
    material = (frequency * frequency).reshape(-1, 1, 1, 1, 1, 1) * permittivity[None, :, None]

    def operate(values):
        above_x = shifted(values[:, :, :, :1], "gx", -1)
        above_y = shifted(values[:, :, :, :, :1], "gy", -1)
        extended = jnp.concatenate([values, above_x], axis=3)
        side_cells = jnp.concatenate([above_y, jnp.zeros_like(above_y[:, :, :, :1])], axis=3)
        extended = jnp.concatenate([extended, side_cells], axis=4)
        rotated = curl_forward(extended, front_x, front_y, front_z)
        below_x = shifted(rotated[:, :, :, -1:], "gx", 1)
        below_y = shifted(rotated[:, :, :, :, -1:], "gy", 1)
        padded = jnp.concatenate([below_x, rotated], axis=3)
        side_cells = jnp.concatenate([jnp.zeros_like(below_y[:, :, :, :1]), below_y], axis=3)
        padded = jnp.concatenate([side_cells, padded], axis=4)
        applied = curl_backward(padded, back_x, back_y, back_z)
        return applied - material * values

    solution = jnp.zeros_like(source)
    residual = source
    direction = source
    shadow_dot = lax.psum(product(source, residual), ("gx", "gy"))
    for iteration in range(ITERS):
        applied = operate(direction)
        step_size = complex_ratio(shadow_dot, lax.psum(product(source, applied), ("gx", "gy")))
        middle = residual - scaled(applied, step_size)
        second = operate(middle)
        sums_triple = lax.psum(
            (product(second, middle), product(second, second), product(source, second)),
            ("gx", "gy"),
        )
        weight = complex_ratio(sums_triple[0], sums_triple[1])
        solution = solution + scaled(direction, step_size) + scaled(middle, weight)
        residual = middle - scaled(second, weight)
        if iteration + 1 < ITERS:
            shadow_next = -complex_times(weight, sums_triple[2])
            momentum = complex_times(
                complex_ratio(shadow_next, shadow_dot), complex_ratio(step_size, weight)
            )
            direction = residual + scaled(direction - scaled(applied, weight), momentum)
            shadow_dot = shadow_next
    return (solution, residual)


def solution(mesh):
    placed = (P("groups", None, None, "gx", "gy", None), P("groups", "gx", "gy", None), P())
    return jax.shard_map(
        body,
        mesh=mesh,
        in_specs=placed,
        out_specs=(
            P("groups", None, None, "gx", "gy", None),
            P("groups", None, None, "gx", "gy", None),
        ),
        check_vma=False,
    )
```

profile of v0, /device:TPU:0, one launch (start us, length us, event | category | flops | bytes accessed | tf_op | source)
XLA Modules:
  0.0 469.3 jit_solution(13969787863053648633)
XLA Ops:
  7.5 6.7 %collective-permute-done = f32[1,3,2,1,32,256]{5,4,3,2,1,0:T(8,128)S(1)} collective-permute-done((f32[1,3,2,1,32,256]{5,4,3,2,1,0:T(8,128)S(1)}, f32[1,3,2,1,32,256]{5,4,3,2,1,0:T(8,128)S(1)}, u32[]{:S(2)}, u32[]{:S(2)}) %collective-permute-start) | collective-permute-done | bytes 196640 | tf_op jit(solution)/shard_map/ppermute | solution.py:17
  15.4 2.2 collective-permute-start.2
  17.5 5.0 %collective-permute-start.3 = (f32[1,3,2,1,32,256]{5,4,3,2,1,0:T(8,128)S(1)}, f32[1,3,2,1,32,256]{5,4,3,2,1,0:T(8,128)S(1)}, u32[]{:S(2)}, u32[]{:S(2)}) collective-permute-start(f32[1,3,2,1,32,256]{5,4,3,2,1,0:T(8,128)S(1)} %pad_maximum_fusion.33), channel_id=1, source_target_pairs={{0,2},{2,4},{4,6},{6,8},{8,10},{10,12},{12,14},{1,3},{3,5},{5,7},{... | collective-permute-start | bytes 589832 | tf_op jit(solution)/shard_map/ppermute | solution.py:17
  22.5 3.6 collective-permute-done.3
  31.1 31.3 %all-reduce.39 = (f32[2,1]{1,0:T(2,128)S(1)}, f32[2,1]{1,0:T(2,128)S(1)}) all-reduce(f32[2,1]{1,0:T(2,128)S(1)} %pad_maximum_fusion.41, f32[2,1]{1,0:T(2,128)S(1)} %pad_maximum_fusion.42), channel_id=1, replica_groups=mesh['groups'=2,'gx'=8,'gy'=2] {'gx','gy'}, use_global_device_ids=true, to_apply=%region_2.0 | all-reduce | flops 4 | bytes 32 | tf_op jit(solution)/shard_map/psum | solution.py:156
  75.6 1.8 collective-permute-done.5
  77.4 3.2 collective-permute-done.4
  94.9 29.5 %all-reduce.38 = (f32[2,1]{1,0:T(2,128)S(1)}, f32[2,1]{1,0:T(2,128)S(1)}, f32[2,1]{1,0:T(2,128)S(1)}) all-reduce(f32[2,1]{1,0:T(2,128)S(1)} %pad_maximum_fusion.43, f32[2,1]{1,0:T(2,128)S(1)} %pad_maximum_fusion.44, f32[2,1]{1,0:T(2,128)S(1)} %pad_maximum_fusion.45), channel_id=1, replica_groups=mesh['groups'=2,'gx'=8,'gy'=2] {'gx','gy'}, use_global_device_ids=true, to_apply=%region_8.0 | all-reduce | flops 6 | bytes 48 | tf_op jit(solution)/shard_map/psum | solution.py:162
  141.5 2.5 multiply_subtract_fusion.11
  168.3 4.2 collective-permute-done.8
  183.4 30.3 %psum.89 = f32[2,1]{1,0:T(2,128)S(1)} all-reduce(f32[2,1]{1,0:T(2,128)S(1)} %pad_maximum_fusion.46), channel_id=1, replica_groups=mesh['groups'=2,'gx'=8,'gy'=2] {'gx','gy'}, use_global_device_ids=true, to_apply=%region_17.0 | all-reduce | flops 2 | bytes 16 | tf_op jit(solution)/shard_map/psum | solution.py:159
  222.7 2.5 multiply_subtract_fusion.8
  230.0 3.4 collective-permute-done.12
  247.5 1.9 pad_maximum_fusion.48
  249.4 1.9 pad_maximum_fusion.47
  251.3 30.6 %all-reduce.37 = (f32[2,1]{1,0:T(2,128)}, f32[2,1]{1,0:T(2,128)}, f32[2,1]{1,0:T(2,128)}) all-reduce(f32[2,1]{1,0:T(2,128)} %pad_maximum_fusion.47, f32[2,1]{1,0:T(2,128)} %pad_maximum_fusion.48, f32[2,1]{1,0:T(2,128)} %pad_maximum_fusion.49), channel_id=1, replica_groups=mesh['groups'=2,'gx'=8,'gy'=2] {'gx','gy'}, use_global_device_ids=true, to_apply=%region_20.0 | all-reduce | flops 6 | bytes 48 | tf_op jit(solution)/shard_map/psum | solution.py:162
  300.1 2.5 multiply_subtract_fusion.5
  327.7 3.7 collective-permute-done.16
  342.3 3.0 add_reduce_fusion.2
  345.3 1.8 pad_maximum_fusion.50
  347.1 2.3 multiply_subtract_fusion.13
  349.4 30.0 %psum.93 = f32[2,1]{1,0:T(2,128)S(1)} all-reduce(f32[2,1]{1,0:T(2,128)} %pad_maximum_fusion.50), channel_id=1, replica_groups=mesh['groups'=2,'gx'=8,'gy'=2] {'gx','gy'}, use_global_device_ids=true, to_apply=%region_29.0 | all-reduce | flops 2 | bytes 16 | tf_op jit(solution)/shard_map/psum | solution.py:159
  388.2 2.5 multiply_subtract_fusion.2
  390.7 2.3 maximum_subtract_fusion.11
  395.6 2.3 multiply_subtract_fusion.9
  397.9 5.9 %collective-permute-done.20 = f32[1,3,2,1,32,256]{5,4,3,2,1,0:T(8,128)S(1)} collective-permute-done((f32[1,3,2,1,32,256]{5,4,3,2,1,0:T(8,128)S(1)}, f32[1,3,2,1,32,256]{5,4,3,2,1,0:T(8,128)S(1)}, u32[]{:S(2)}, u32[]{:S(2)}) %collective-permute-start.20) | collective-permute-done | bytes 196640 | tf_op jit(solution)/shard_map/ppermute | solution.py:17
  405.4 2.0 collective-permute-start.22
  407.5 1.9 collective-permute-start.23
  409.3 2.2 multiply_subtract_fusion.7
  420.7 2.2 multiply_subtract_fusion.3
  422.9 29.5 %all-reduce.36 = (f32[2,1]{1,0:T(2,128)S(1)}, f32[2,1]{1,0:T(2,128)S(1)}) all-reduce(f32[2,1]{1,0:T(2,128)S(1)} %pad_maximum_fusion.51, f32[2,1]{1,0:T(2,128)S(1)} %pad_maximum_fusion.52), channel_id=1, replica_groups=mesh['groups'=2,'gx'=8,'gy'=2] {'gx','gy'}, use_global_device_ids=true, to_apply=%region_32.0 | all-reduce | flops 4 | bytes 32 | tf_op jit(solution)/shard_map/psum | solution.py:162
  461.4 2.6 multiply_subtract_fusion
  (455 shorter events, 112.2 us)
Async XLA Ops:
  1.6 12.5 %collective-permute-start.1 = (f32[1,3,2,4,1,256]{5,4,3,2,1,0:T(1,128)S(1)}, f32[1,3,2,4,1,256]{5,4,3,2,1,0:T(1,128)S(1)}, u32[]{:S(2)}, u32[]{:S(2)}) collective-permute-start(f32[1,3,2,4,1,256]{5,4,3,2,1,0:T(1,128)S(1)} %slice.702), channel_id=1, source_target_pairs={{1,0},{3,2},{5,4},{7,6},{9,8},{11,10},{13,12},{15,14},{17,16},{19,... | collective-permute-start | bytes 73736 | tf_op jit(solution)/shard_map/ppermute | solution.py:17
  3.9 10.2 %collective-permute-start = (f32[1,3,2,1,32,256]{5,4,3,2,1,0:T(8,128)S(1)}, f32[1,3,2,1,32,256]{5,4,3,2,1,0:T(8,128)S(1)}, u32[]{:S(2)}, u32[]{:S(2)}) collective-permute-start(f32[1,3,2,1,32,256]{5,4,3,2,1,0:T(8,128)S(1)} %slice.695), channel_id=1, source_target_pairs={{2,0},{4,2},{6,4},{8,6},{10,8},{12,10},{14,12},{3,1},{5,3},{7,5},{... | collective-permute-start | bytes 589832 | tf_op jit(solution)/shard_map/ppermute | solution.py:17
  7.1 172.1 %copy-start.53 = (f32[4]{0:T(128)}, f32[4]{0:T(128)S(1)}, u32[]{:S(2)}) copy-start(f32[4]{0:T(128)S(1)} %get-tuple-element.424) | copy-start | bytes 52
  7.1 172.1 %copy-start.57 = (f32[4]{0:T(128)}, f32[4]{0:T(128)S(1)}, u32[]{:S(2)}) copy-start(f32[4]{0:T(128)S(1)} %get-tuple-element.425) | copy-start | bytes 52
  7.2 166.2 %copy-start.61 = (f32[4]{0:T(128)}, f32[4]{0:T(128)S(1)}, u32[]{:S(2)}) copy-start(f32[4]{0:T(128)S(1)} %get-tuple-element.432) | copy-start | bytes 52
  7.2 166.2 %copy-start.65 = (f32[4]{0:T(128)}, f32[4]{0:T(128)S(1)}, u32[]{:S(2)}) copy-start(f32[4]{0:T(128)S(1)} %get-tuple-element.433) | copy-start | bytes 52
  7.4 172.3 %copy-start.16 = (f32[3,4,32,256]{3,2,1,0:T(8,128)}, f32[3,4,32,256]{3,2,1,0:T(8,128)S(1)}, u32[]{:S(2)}) copy-start(f32[3,4,32,256]{3,2,1,0:T(8,128)S(1)} %broadcast_multiply_fusion) | copy-start | bytes 1179652
  7.4 165.7 %copy-start.77 = (f32[32]{0:T(128)}, f32[32]{0:T(128)S(1)}, u32[]{:S(2)}) copy-start(f32[32]{0:T(128)S(1)} %get-tuple-element.430) | copy-start | bytes 388
  7.4 165.7 %copy-start.81 = (f32[32]{0:T(128)}, f32[32]{0:T(128)S(1)}, u32[]{:S(2)}) copy-start(f32[32]{0:T(128)S(1)} %get-tuple-element.431) | copy-start | bytes 388
  15.4 7.2 %collective-permute-start.2 = (f32[1,3,2,4,1,256]{5,4,3,2,1,0:T(1,128)S(1)}, f32[1,3,2,4,1,256]{5,4,3,2,1,0:T(1,128)S(1)}, u32[]{:S(2)}, u32[]{:S(2)}) collective-permute-start(f32[1,3,2,4,1,256]{5,4,3,2,1,0:T(1,128)S(1)} %pad_maximum_fusion.40), channel_id=1, source_target_pairs={{0,1},{2,3},{4,5},{6,7},{8,9},{10,11},{12,13},{14,15},{16,17},{18,... | collective-permute-start | bytes 73736 | tf_op jit(solution)/shard_map/ppermute | solution.py:17
  17.5 8.7 %collective-permute-start.3 = (f32[1,3,2,1,32,256]{5,4,3,2,1,0:T(8,128)S(1)}, f32[1,3,2,1,32,256]{5,4,3,2,1,0:T(8,128)S(1)}, u32[]{:S(2)}, u32[]{:S(2)}) collective-permute-start(f32[1,3,2,1,32,256]{5,4,3,2,1,0:T(8,128)S(1)} %pad_maximum_fusion.33), channel_id=1, source_target_pairs={{0,2},{2,4},{4,6},{6,8},{8,10},{10,12},{12,14},{1,3},{3,5},{5,7},{... | collective-permute-start | bytes 589832 | tf_op jit(solution)/shard_map/ppermute | solution.py:17
  22.5 156.8 %copy-start.69 = (f32[32]{0:T(128)}, f32[32]{0:T(128)S(1)}, u32[]{:S(2)}) copy-start(f32[32]{0:T(128)S(1)} %get-tuple-element.422) | copy-start | bytes 388
  73.0 7.6 %collective-permute-start.4 = (f32[1,3,2,1,32,256]{5,4,3,2,1,0:T(8,128)S(1)}, f32[1,3,2,1,32,256]{5,4,3,2,1,0:T(8,128)S(1)}, u32[]{:S(2)}, u32[]{:S(2)}) collective-permute-start(f32[1,3,2,1,32,256]{5,4,3,2,1,0:T(8,128)S(1)} %slice.2127), channel_id=1, source_target_pairs={{2,0},{4,2},{6,4},{8,6},{10,8},{12,10},{14,12},{3,1},{5,3},{7,5},{... | collective-permute-start | bytes 589832 | tf_op jit(solution)/shard_map/ppermute | solution.py:17
  74.3 3.1 collective-permute-start.5
  81.7 5.9 %collective-permute-start.7 = (f32[1,3,2,1,32,256]{5,4,3,2,1,0:T(8,128)S(1)}, f32[1,3,2,1,32,256]{5,4,3,2,1,0:T(8,128)S(1)}, u32[]{:S(2)}, u32[]{:S(2)}) collective-permute-start(f32[1,3,2,1,32,256]{5,4,3,2,1,0:T(8,128)S(1)} %pad_maximum_fusion.31), channel_id=1, source_target_pairs={{0,2},{2,4},{4,6},{6,8},{8,10},{10,12},{12,14},{1,3},{3,5},{5,7},{... | collective-permute-start | bytes 589832 | tf_op jit(solution)/shard_map/ppermute | solution.py:17
  83.2 4.4 collective-permute-start.6
  163.9 8.6 %collective-permute-start.8 = (f32[1,3,2,1,32,256]{5,4,3,2,1,0:T(8,128)S(1)}, f32[1,3,2,1,32,256]{5,4,3,2,1,0:T(8,128)S(1)}, u32[]{:S(2)}, u32[]{:S(2)}) collective-permute-start(f32[1,3,2,1,32,256]{5,4,3,2,1,0:T(8,128)S(1)} %slice.2170), channel_id=1, source_target_pairs={{2,0},{4,2},{6,4},{8,6},{10,8},{12,10},{14,12},{3,1},{5,3},{7,5},{... | collective-permute-start | bytes 589832 | tf_op jit(solution)/shard_map/ppermute | solution.py:17
  165.2 3.1 collective-permute-start.9
  173.6 4.9 %collective-permute-start.11 = (f32[1,3,2,1,32,256]{5,4,3,2,1,0:T(8,128)S(1)}, f32[1,3,2,1,32,256]{5,4,3,2,1,0:T(8,128)S(1)}, u32[]{:S(2)}, u32[]{:S(2)}) collective-permute-start(f32[1,3,2,1,32,256]{5,4,3,2,1,0:T(8,128)S(1)} %pad_maximum_fusion.29), channel_id=1, source_target_pairs={{0,2},{2,4},{4,6},{6,8},{8,10},{10,12},{12,14},{1,3},{3,5},{5,7},{... | collective-permute-start | bytes 589832 | tf_op jit(solution)/shard_map/ppermute | solution.py:17
  175.1 2.1 collective-permute-start.10
  225.6 7.8 %collective-permute-start.12 = (f32[1,3,2,1,32,256]{5,4,3,2,1,0:T(8,128)S(1)}, f32[1,3,2,1,32,256]{5,4,3,2,1,0:T(8,128)S(1)}, u32[]{:S(2)}, u32[]{:S(2)}) collective-permute-start(f32[1,3,2,1,32,256]{5,4,3,2,1,0:T(8,128)S(1)} %slice.2211), channel_id=1, source_target_pairs={{2,0},{4,2},{6,4},{8,6},{10,8},{12,10},{14,12},{3,1},{5,3},{7,5},{... | collective-permute-start | bytes 589832 | tf_op jit(solution)/shard_map/ppermute | solution.py:17
  226.9 3.1 collective-permute-start.13
  235.0 5.6 %collective-permute-start.15 = (f32[1,3,2,1,32,256]{5,4,3,2,1,0:T(8,128)S(1)}, f32[1,3,2,1,32,256]{5,4,3,2,1,0:T(8,128)S(1)}, u32[]{:S(2)}, u32[]{:S(2)}) collective-permute-start(f32[1,3,2,1,32,256]{5,4,3,2,1,0:T(8,128)S(1)} %pad_maximum_fusion.27), channel_id=1, source_target_pairs={{0,2},{2,4},{4,6},{6,8},{8,10},{10,12},{12,14},{1,3},{3,5},{5,7},{... | collective-permute-start | bytes 589832 | tf_op jit(solution)/shard_map/ppermute | solution.py:17
  236.5 4.0 collective-permute-start.14
  323.3 8.1 %collective-permute-start.16 = (f32[1,3,2,1,32,256]{5,4,3,2,1,0:T(8,128)S(1)}, f32[1,3,2,1,32,256]{5,4,3,2,1,0:T(8,128)S(1)}, u32[]{:S(2)}, u32[]{:S(2)}) collective-permute-start(f32[1,3,2,1,32,256]{5,4,3,2,1,0:T(8,128)S(1)} %slice.2254), channel_id=1, source_target_pairs={{2,0},{4,2},{6,4},{8,6},{10,8},{12,10},{14,12},{3,1},{5,3},{7,5},{... | collective-permute-start | bytes 589832 | tf_op jit(solution)/shard_map/ppermute | solution.py:17
  324.6 3.1 collective-permute-start.17
  333.0 5.3 %collective-permute-start.19 = (f32[1,3,2,1,32,256]{5,4,3,2,1,0:T(8,128)S(1)}, f32[1,3,2,1,32,256]{5,4,3,2,1,0:T(8,128)S(1)}, u32[]{:S(2)}, u32[]{:S(2)}) collective-permute-start(f32[1,3,2,1,32,256]{5,4,3,2,1,0:T(8,128)S(1)} %pad_maximum_fusion.25), channel_id=1, source_target_pairs={{0,2},{2,4},{4,6},{6,8},{8,10},{10,12},{12,14},{1,3},{3,5},{5,7},{... | collective-permute-start | bytes 589832 | tf_op jit(solution)/shard_map/ppermute | solution.py:17
  334.6 2.1 collective-permute-start.18
  393.0 5.0 %collective-permute-start.21 = (f32[1,3,2,4,1,256]{5,4,3,2,1,0:T(1,128)S(1)}, f32[1,3,2,4,1,256]{5,4,3,2,1,0:T(1,128)S(1)}, u32[]{:S(2)}, u32[]{:S(2)}) collective-permute-start(f32[1,3,2,4,1,256]{5,4,3,2,1,0:T(1,128)S(1)} %slice.2299), channel_id=1, source_target_pairs={{1,0},{3,2},{5,4},{7,6},{9,8},{11,10},{13,12},{15,14},{17,16},{19,... | collective-permute-start | bytes 73736 | tf_op jit(solution)/shard_map/ppermute | solution.py:17
  394.3 9.5 %collective-permute-start.20 = (f32[1,3,2,1,32,256]{5,4,3,2,1,0:T(8,128)S(1)}, f32[1,3,2,1,32,256]{5,4,3,2,1,0:T(8,128)S(1)}, u32[]{:S(2)}, u32[]{:S(2)}) collective-permute-start(f32[1,3,2,1,32,256]{5,4,3,2,1,0:T(8,128)S(1)} %slice.2295), channel_id=1, source_target_pairs={{2,0},{4,2},{6,4},{8,6},{10,8},{12,10},{14,12},{3,1},{5,3},{7,5},{... | collective-permute-start | bytes 589832 | tf_op jit(solution)/shard_map/ppermute | solution.py:17
  405.4 6.1 %collective-permute-start.22 = (f32[1,3,2,4,1,256]{5,4,3,2,1,0:T(1,128)S(1)}, f32[1,3,2,4,1,256]{5,4,3,2,1,0:T(1,128)S(1)}, u32[]{:S(2)}, u32[]{:S(2)}) collective-permute-start(f32[1,3,2,4,1,256]{5,4,3,2,1,0:T(1,128)S(1)} %pad_maximum_fusion.35), channel_id=1, source_target_pairs={{0,1},{2,3},{4,5},{6,7},{8,9},{10,11},{12,13},{14,15},{16,17},{18,... | collective-permute-start | bytes 73736 | tf_op jit(solution)/shard_map/ppermute | solution.py:17
  407.5 5.3 %collective-permute-start.23 = (f32[1,3,2,1,32,256]{5,4,3,2,1,0:T(8,128)S(1)}, f32[1,3,2,1,32,256]{5,4,3,2,1,0:T(8,128)S(1)}, u32[]{:S(2)}, u32[]{:S(2)}) collective-permute-start(f32[1,3,2,1,32,256]{5,4,3,2,1,0:T(8,128)S(1)} %pad_maximum_fusion.23), channel_id=1, source_target_pairs={{0,2},{2,4},{4,6},{6,8},{8,10},{10,12},{12,14},{1,3},{3,5},{5,7},{... | collective-permute-start | bytes 589832 | tf_op jit(solution)/shard_map/ppermute | solution.py:17
  (78 other events, 651.4 us)
where the time goes:
time: 472 us; the launch traced here: 469 us
  blocking collectives  181 us (38%)
  between operations  99.9 us (21%)
  other arithmetic  74.5 us (16%)
  waiting for transfers between devices  43.6 us (9%)
  starting transfers between devices  38.4 us (8%)
  local copies, waits for them, and re-layouts  31.8 us (7%)
    psum x3, blocking collectives, body(): lax.psum((product(second, middle), product(second, second), product(sourc...  89.6 us
    psum x2, blocking collectives, body(): lax.psum(product(source, applied), ('gx', 'gy'))  60.3 us
    ppermute x24, waiting for transfers between devices, shifted(): return lax.ppermute(array, axis, pairs)  43.6 us
    ppermute x24, starting transfers between devices, shifted(): return lax.ppermute(array, axis, pairs)  38.4 us
    psum x1, blocking collectives, body(): shadow_dot = lax.psum(product(source, residual), ('gx', 'gy'))  31.3 us
    sub x15, other arithmetic, scaled(): real_part = values[:, :, 0] * real_scale - values[:, :, 1] * imag_scale  27.3 us
    another operation x12, other arithmetic, product(): return jnp.stack([real_part, imag_part])  17.5 us
    unnamed x173, local copies, waits for them, and re-layouts  12.9 us
  transfers between devices with their start and end apart: 24, of which 17 were waited for; matrix products, arithmetic and copies ran while one was open for 2% of the time, Pallas kernels for 0%

commit v1 on v0

v1 whole, which is shorter than its diff:
```python
import functools

import jax
import jax.numpy as jnp
from jax import lax
from jax.experimental import pallas as pl
from jax.experimental.pallas import tpu as pltpu
from jax.sharding import PartitionSpec as P

PML = 8
ITERS = 3
STEPS = 2 * ITERS
SLOTS = 8
CENTRE = 4.0
HALF = 8.0
LANES = 128
pml_strength = 2.0

DOWN, UP, Y_DOWN, Y_UP, DIAG_DOWN, DIAG_UP = range(6)


def stretch(points, length, frequency):
    inside = jnp.maximum(jnp.maximum(PML - points, points - (length - PML)), 0.0) / PML
    damping = pml_strength * inside * inside * inside / frequency
    factor = 1.0 / (1.0 + damping * damping)
    return factor, -damping * factor


def cmul(a, b):
    return a[0] * b[0] - a[1] * b[1], a[0] * b[1] + a[1] * b[0]


def cadd(a, b):
    return a[0] + b[0], a[1] + b[1]


def csub(a, b):
    return a[0] - b[0], a[1] - b[1]


def cdiv(a, b):
    modulus = b[0] * b[0] + b[1] * b[1]
    return (a[0] * b[0] + a[1] * b[1]) / modulus, (a[1] * b[0] - a[0] * b[1]) / modulus


def kernel(sizes, src, eps, freq, x_out, r_out, V, mat, H, recv_e, recv_p, send_p, recv_yd,
           recv_yu, send_yd, send_yu, recv_dd, recv_du, send_dd, send_du, hrow, fxt, bxt, fyt,
           byt, fym, fzt, bzt, gram, send_g, recv_g, coef, send_sem, recv_sem, gsend_sem,
           grecv_sem, local_sem):
    gx_n, gy_n = sizes
    X, Y, Z = V.shape[3:]
    gx, gy = lax.axis_index("gx"), lax.axis_index("gy")
    frequency = freq[0]
    first_x, last_x = gx == 0, gx == gx_n - 1
    first_y, last_y = gy == 0, gy == gy_n - 1
    devices = gx_n * gy_n
    me = gx * gy_n + gy

    load_src = pltpu.make_async_copy(src, V.at[0], local_sem.at[0])
    load_eps = pltpu.make_async_copy(eps, mat, local_sem.at[1])
    load_src.start()
    load_eps.start()

    barrier = pltpu.get_barrier_semaphore()

    def greet(d, carry):
        other = lax.rem(me + d, devices)
        pl.semaphore_signal(
            barrier, inc=1, device_id={"gx": other // gy_n, "gy": lax.rem(other, gy_n)},
            device_id_type=pl.DeviceIdType.MESH)
        return carry

    lax.fori_loop(1, devices, greet, 0)

    def fill(ref, pair):
        ref[0] = pair[0]
        ref[1] = pair[1]

    def iota(shape, dim):
        return lax.broadcasted_iota(jnp.int32, shape, dim)

    rows_x = fxt.shape[1]
    px = (gx * X - 1 + iota((rows_x, Z), 0)).astype(jnp.float32) + 0.5
    front = stretch(px, X * gx_n, frequency)
    keep = jnp.logical_or(iota((rows_x, Z), 0) > 0, jnp.full((rows_x, Z), gx, jnp.int32) > 0)
    fill(fxt, [jnp.where(keep, f, 0.0) for f in front])
    px = (gx * X + iota((rows_x, Z), 0)).astype(jnp.float32)
    fill(bxt, stretch(px, X * gx_n, frequency))
    py = (gy * Y + iota((Y, Z), 0)).astype(jnp.float32)
    fill(fyt, stretch(py + 0.5, Y * gy_n, frequency))
    fill(byt, stretch(py, Y * gy_n, frequency))
    pm = (gy * Y - 1 + iota((8, Z), 0)).astype(jnp.float32) + 0.5
    keep = jnp.full((8, Z), gy, jnp.int32) > 0
    fill(fym, [jnp.where(keep, f, 0.0) for f in stretch(pm, Y * gy_n, frequency)])
    pz = iota((8, Z), 1).astype(jnp.float32)
    fill(fzt, stretch(pz + 0.5, Z, frequency))
    fill(bzt, stretch(pz, Z, frequency))

    @pl.when(last_x)
    def _():
        recv_e[...] = jnp.zeros_like(recv_e)

    @pl.when(first_x)
    def _():
        recv_p[...] = jnp.zeros_like(recv_p)

    @pl.when(last_y)
    def _():
        recv_yd[...] = jnp.zeros_like(recv_yd)

    @pl.when(first_y)
    def _():
        recv_yu[...] = jnp.zeros_like(recv_yu)

    @pl.when(jnp.logical_or(last_x, first_y))
    def _():
        recv_dd[...] = jnp.zeros_like(recv_dd)

    @pl.when(jnp.logical_or(first_x, last_y))
    def _():
        recv_du[...] = jnp.zeros_like(recv_du)

    gram[...] = jnp.zeros_like(gram)

    def copy(kind, k, source, target, dx, dy):
        return pltpu.make_async_remote_copy(
            src_ref=source, dst_ref=target, send_sem=send_sem.at[kind, k],
            recv_sem=recv_sem.at[kind, k], device_id={"gx": gx + dx, "gy": gy + dy},
            device_id_type=pl.DeviceIdType.MESH)

    def messages(k):
        return {
            DOWN: (lambda: copy(DOWN, k, V.at[k, 1:3, :, 0], recv_e.at[k], -1, 0),
                   gx > 0, gx < gx_n - 1),
            UP: (lambda: copy(UP, k, send_p.at[k], recv_p.at[k], 1, 0),
                 gx < gx_n - 1, gx > 0),
            Y_DOWN: (lambda: copy(Y_DOWN, k, send_yd.at[k], recv_yd.at[k], 0, -1),
                     gy > 0, gy < gy_n - 1),
            Y_UP: (lambda: copy(Y_UP, k, send_yu.at[k], recv_yu.at[k], 0, 1),
                   gy < gy_n - 1, gy > 0),
            DIAG_DOWN: (lambda: copy(DIAG_DOWN, k, send_dd.at[k], recv_dd.at[k], -1, 1),
                        jnp.logical_and(gx > 0, gy < gy_n - 1),
                        jnp.logical_and(gx < gx_n - 1, gy > 0)),
            DIAG_UP: (lambda: copy(DIAG_UP, k, send_du.at[k], recv_du.at[k], 1, -1),
                      jnp.logical_and(gx < gx_n - 1, gy > 0),
                      jnp.logical_and(gx > 0, gy < gy_n - 1)),
        }

    def send(k, kind):
        message, sends, _ = messages(k)[kind]
        pl.when(sends)(lambda: message().start())

    def receive(k, kind):
        message, _, receives = messages(k)[kind]
        pl.when(receives)(lambda: message().wait_recv())

    def row(ref, index):
        return ref[0, pl.ds(index, 1)], ref[1, pl.ds(index, 1)]

    def whole(ref):
        return ref[0], ref[1]

    def next_z(values):
        rolled = pltpu.roll(values, Z - 1, 1)
        return jnp.where(iota(values.shape, 1) == Z - 1, 0.0, rolled)

    def prev_z(values):
        rolled = pltpu.roll(values, 1, 1)
        return jnp.where(iota(values.shape, 1) == 0, 0.0, rolled)

    def next_y(values, edge):
        rolled = pltpu.roll(values, Y - 1, 0)
        return jnp.where(iota(values.shape, 0) == Y - 1, edge, rolled)

    def prev_y(values, edge):
        rolled = pltpu.roll(values, 1, 0)
        return jnp.where(iota(values.shape, 0) == 0, edge, rolled)

    def both(f, *pairs):
        return tuple(f(*[p[i] for p in pairs]) for i in range(2))

    def front_dz(pair):
        return cmul(both(lambda a: next_z(a) - a, pair), row(fzt, 0))

    def back_dz(pair):
        return cmul(both(lambda a: a - prev_z(a), pair), row(bzt, 0))

    def cell(k, component, x):
        return V[k, component, 0, x], V[k, component, 1, x]

    def cells_at(k, component, y):
        return V[k, component, 0, :, y, :], V[k, component, 1, :, y, :]

    zero_row = jnp.zeros((1, Z), jnp.float32)

    def dots(k):
        def one(j, carry):
            re = jnp.zeros((Y, Z), jnp.float32)
            im = jnp.zeros((Y, Z), jnp.float32)
            for component in range(3):
                for x in range(X):
                    a, b = cell(j, component, x), cell(k, component, x)
                    re = re + (a[0] * b[0] + a[1] * b[1])
                    im = im + (a[0] * b[1] - a[1] * b[0])

            def fold(values):
                values = jnp.sum(values, axis=0, keepdims=True)
                return sum(values[:, i:i + LANES] for i in range(0, Z, LANES))

            re, im = fold(re), fold(im)
            gram[pl.ds(j * SLOTS + k, 1)] = re
            gram[pl.ds(k * SLOTS + j, 1)] = re
            gram[pl.ds((SLOTS + j) * SLOTS + k, 1)] = im
            gram[pl.ds((SLOTS + k) * SLOTS + j, 1)] = -im
            return carry

        lax.fori_loop(0, k + 1, one, 0)

    def h_layer(k, x, above_y, above_z):
        ex, ey, ez = cell(k, 0, x), cell(k, 1, x), cell(k, 2, x)
        fx, fy = row(fxt, x + 1), whole(fyt)
        ez_edge = recv_yd[k, 1, 0, pl.ds(x, 1)], recv_yd[k, 1, 1, pl.ds(x, 1)]
        ex_edge = recv_yd[k, 0, 0, pl.ds(x, 1)], recv_yd[k, 0, 1, pl.ds(x, 1)]

        def dy(pair, edge):
            return cmul(both(lambda a, e: next_y(a, e) - a, pair, edge), fy)

        hx = csub(dy(ez, ez_edge), front_dz(ey))
        hy = csub(front_dz(ex), cmul(csub(above_z, ez), fx))
        hz = csub(cmul(csub(above_y, ey), fx), dy(ex, ex_edge))
        for component, pair in enumerate((hx, hy, hz)):
            for part in range(2):
                H[component, part, x] = pair[part]

    def hcell(component, x):
        return H[component, 0, x], H[component, 1, x]

    def out_layer(k, x, below_y, below_z, a_k, b_k):
        hx, hy, hz = hcell(0, x), hcell(1, x), hcell(2, x)
        bx, by = row(bxt, x), whole(byt)
        hx_edge = hrow[0, 0, pl.ds(x, 1)], hrow[0, 1, pl.ds(x, 1)]
        hz_edge = hrow[1, 0, pl.ds(x, 1)], hrow[1, 1, pl.ds(x, 1)]

        def dy(pair, edge):
            return cmul(both(lambda a, e: a - prev_y(a, e), pair, edge), by)

        cx = csub(dy(hz, hz_edge), back_dz(hy))
        cy = csub(back_dz(hx), cmul(csub(hz, below_z), bx))
        cz = csub(cmul(csub(hy, below_y), bx), dy(hx, hx_edge))
        before = jnp.maximum(k - 1, 0)
        for component, pair in enumerate((cx, cy, cz)):
            material = mat[component, x]
            for part in range(2):
                value = a_k * (pair[part] - material * V[k, component, part, x])
                V[k + 1, component, part, x] = value - b_k * V[before, component, part, x]

    def step(k, carry):
        a_k = jnp.where(k == 0, 1.0 / HALF, 2.0 / HALF).astype(jnp.float32)
        b_k = jnp.where(k == 0, 0.0, 1.0).astype(jnp.float32)
        top = X - 1

        for part in range(2):
            send_dd[k, pl.ds(part, 1)] = V[k, 1, part, 0, pl.ds(Y - 1, 1)]
            send_du[k, pl.ds(part, 1)] = V[k, 0, part, top, pl.ds(0, 1)]
            for i, component in enumerate((0, 2)):
                for x in range(X):
                    send_yd[k, i, part, pl.ds(x, 1)] = V[k, component, part, x, pl.ds(0, 1)]
        send(k, DIAG_DOWN)
        send(k, DIAG_UP)
        send(k, Y_DOWN)
        send(k, DOWN)

        ex, ey, ez = cell(k, 0, top), cell(k, 1, top), cell(k, 2, top)
        fx = row(fxt, X)
        fy = whole(fyt)
        py_ = cadd(front_dz(ex), cmul(ez, fx))
        dy = cmul(both(lambda a: next_y(a, zero_row) - a, ex), fy)
        pz_ = cadd(cmul(ey, fx), dy)
        for part in range(2):
            send_p[k, 0, part] = py_[part]
            send_p[k, 1, part] = -pz_[part]
        send(k, UP)

        fy = row(fyt, Y - 1)
        for x in range(X):
            at = pl.ds(Y - 1, 1)
            ex, ey, ez = ((V[k, c, 0, x, at], V[k, c, 1, x, at]) for c in range(3))
            if x < top:
                ahead = V[k, 1, 0, x + 1, at], V[k, 1, 1, x + 1, at]
            else:
                ahead = zero_row, zero_row
            qx = cadd(cmul(ez, fy), front_dz(ey))
            qz = cadd(cmul(csub(ahead, ey), row(fxt, x + 1)), cmul(ex, fy))
            for part in range(2):
                send_yu[k, 0, part, pl.ds(x, 1)] = -qx[part]
                send_yu[k, 1, part, pl.ds(x, 1)] = qz[part]
        send(k, Y_UP)

        receive(k, Y_DOWN)
        for x in range(X - 1):
            h_layer(k, x, cell(k, 1, x + 1), cell(k, 2, x + 1))

        receive(k, Y_UP)
        fm = row(fym, 0)
        for x in range(X):
            at = pl.ds(0, 1)
            ex, ez = ((V[k, c, 0, x, at], V[k, c, 1, x, at]) for c in (0, 2))
            qx = recv_yu[k, 0, 0, pl.ds(x, 1)], recv_yu[k, 0, 1, pl.ds(x, 1)]
            qz = recv_yu[k, 1, 0, pl.ds(x, 1)], recv_yu[k, 1, 1, pl.ds(x, 1)]
            hx, hz = cadd(qx, cmul(ez, fm)), csub(qz, cmul(ex, fm))
            for part in range(2):
                hrow[0, part, pl.ds(x, 1)] = hx[part]
                hrow[1, part, pl.ds(x, 1)] = hz[part]
        for x in range(1, X - 1):
            out_layer(k, x, hcell(1, x - 1), hcell(2, x - 1), a_k, b_k)

        dots(k)

        receive(k, DIAG_DOWN)
        fix = cmul((recv_dd[k, pl.ds(0, 1)], recv_dd[k, pl.ds(1, 1)]), row(fxt, X))
        for part in range(2):
            hrow[1, part, pl.ds(top, 1)] = hrow[1, part, pl.ds(top, 1)] + fix[part]
        receive(k, DOWN)
        h_layer(k, top, (recv_e[k, 0, 0], recv_e[k, 0, 1]), (recv_e[k, 1, 0], recv_e[k, 1, 1]))
        out_layer(k, top, hcell(1, top - 1), hcell(2, top - 1), a_k, b_k)

        receive(k, DIAG_UP)
        receive(k, UP)
        fx = row(fxt, 0)
        hy = csub((recv_p[k, 0, 0], recv_p[k, 0, 1]), cmul(cell(k, 2, 0), fx))
        hz = cadd((recv_p[k, 1, 0], recv_p[k, 1, 1]), cmul(cell(k, 1, 0), fx))
        fix = cmul((recv_du[k, pl.ds(0, 1)], recv_du[k, pl.ds(1, 1)]), row(fyt, Y - 1))
        hz = both(lambda a, f: jnp.where(iota((Y, Z), 0) == Y - 1, a - f, a), hz, fix)
        out_layer(k, 0, hy, hz, a_k, b_k)
        return carry

    load_eps.wait()
    square = frequency * frequency
    for component in range(3):
        for x in range(X):
            mat[component, x] = mat[component, x] * square + CENTRE
    load_src.wait()
    pl.semaphore_wait(barrier, devices - 1)

    lax.fori_loop(0, STEPS, step, 0)
    dots(STEPS)

    sums = jnp.sum(gram[...], axis=1, keepdims=True)
    count = 2 * SLOTS * SLOTS
    spread = jnp.where(iota((count, LANES), 0) == iota((count, LANES), 1), sums, 0.0)
    send_g[...] = jnp.sum(spread, axis=0, keepdims=True)
    recv_g[me] = send_g[...]

    def gram_copy(d, slot):
        other = lax.rem(me + d, devices)
        return pltpu.make_async_remote_copy(
            src_ref=send_g, dst_ref=recv_g.at[slot], send_sem=gsend_sem.at[d],
            recv_sem=grecv_sem.at[slot],
            device_id={"gx": other // gy_n, "gy": lax.rem(other, gy_n)},
            device_id_type=pl.DeviceIdType.MESH)

    def start(d, carry):
        gram_copy(d, me).start()
        return carry

    lax.fori_loop(1, devices, start, 0)

    def finish(d, carry):
        gram_copy(d, lax.rem(me + d, devices)).wait_recv()
        return carry

    lax.fori_loop(1, devices, finish, 0)
    total = jnp.broadcast_to(jnp.sum(recv_g[...], axis=0), (SLOTS, LANES))

    tile = (SLOTS, LANES)
    sub, lane = iota(tile, 0), iota(tile, 1)

    def unpack(start_at):
        out = jnp.zeros(tile, jnp.float32)
        for i in range(SLOTS):
            shift = (LANES - start_at - i * SLOTS) % LANES
            moved = total if shift == 0 else pltpu.roll(total, shift, 1)
            out = jnp.where(sub == i, moved, out)
        return jnp.where(lane < SLOTS, out, 0.0)

    g = unpack(0), unpack(SLOTS * SLOTS)

    def combine(f, *vectors):
        return tuple(f(*[v[i] for v in vectors]) for i in range(2))

    def operate(vector):
        def one(axis, index, size):
            lift = jnp.where(index == 1, 1.0, jnp.where(index == 0, 0.0, 0.5))
            drop = jnp.where(index < SLOTS - 1, 0.5, 0.0)

            def real(p):
                moved = lift * pltpu.roll(p, 1, axis) + drop * pltpu.roll(p, size - 1, axis)
                return CENTRE * p + HALF * moved
            return real

        along, down = vector
        return (both(one(1, lane, LANES), along), both(one(0, sub, SLOTS), down))

    def inner(left, right):
        t = cmul(g, right[0])
        a = left[1]

        def full(values):
            return jnp.sum(jnp.sum(values, axis=1, keepdims=True), axis=0, keepdims=True)

        return full(a[0] * t[0] + a[1] * t[1]), full(a[0] * t[1] - a[1] * t[0])

    def scaled(vector, number):
        return combine(lambda v: cmul(v, number), vector)

    zero = jnp.zeros(tile, jnp.float32)
    unit = ((jnp.where(lane == 0, 1.0, 0.0), zero), (jnp.where(sub == 0, 1.0, 0.0), zero))
    answer = ((zero, zero), (zero, zero))
    residual = direction = unit
    rho = inner(unit, unit)
    for iteration in range(ITERS):
        image = operate(direction)
        alpha = cdiv(rho, inner(unit, image))
        middle = combine(csub, residual, scaled(image, alpha))
        second = operate(middle)
        weight = cdiv(inner(second, middle), inner(second, second))
        answer = combine(cadd, answer, scaled(direction, alpha))
        answer = combine(cadd, answer, scaled(middle, weight))
        residual = combine(csub, middle, scaled(second, weight))
        if iteration + 1 < ITERS:
            moved = cmul(weight, inner(unit, second))
            rho_next = -moved[0], -moved[1]
            beta = cmul(cdiv(rho_next, rho), cdiv(alpha, weight))
            pull = combine(csub, direction, scaled(image, weight))
            direction = combine(cadd, residual, scaled(pull, beta))
            rho = rho_next

    for i, values in enumerate((answer[1][0], answer[1][1], residual[1][0], residual[1][1])):
        for at in range(0, Z, LANES):
            coef[i, :, pl.ds(at, LANES)] = values

    def emit(index, carry):
        component = index // X
        x = lax.rem(index, X)
        for out, base, last in ((x_out, 0, STEPS), (r_out, 2, STEPS + 1)):
            re = im = jnp.zeros((Y, Z), jnp.float32)
            for k in range(last):
                c = coef[base, pl.ds(k, 1)], coef[base + 1, pl.ds(k, 1)]
                v = V[k, component, 0, x], V[k, component, 1, x]
                p = cmul(v, c)
                re, im = re + p[0], im + p[1]
            out[component, 0, x] = re
            out[component, 1, x] = im
        return carry

    lax.fori_loop(0, 3 * X, emit, 0)

    def drain(k, carry):
        for message, sends, _ in messages(k).values():
            pl.when(sends)(lambda: message().wait_send())
        return carry

    lax.fori_loop(0, STEPS, drain, 0)

    def drain_gram(d, carry):
        gram_copy(d, me).wait_send()
        return carry

    lax.fori_loop(1, devices, drain_gram, 0)


def solution(mesh):
    gx_n, gy_n = mesh.shape["gx"], mesh.shape["gy"]
    devices = gx_n * gy_n

    def body(source, permittivity, frequency):
        X, Y, Z = source.shape[3:]
        field = source.shape[1:]
        f32 = jnp.float32
        rows_x = -(-(X + 1) // 8) * 8
        vmem = pltpu.VMEM
        face = (STEPS, 2, 2, Y, Z)
        rows = (STEPS, 2, 2, X, Z)
        diag = (STEPS, 2, Z)
        scratch = [
            vmem((STEPS + 1,) + field, f32), vmem(permittivity.shape, f32), vmem(field, f32),
            vmem(face, f32), vmem(face, f32), vmem(face, f32),
            vmem(rows, f32), vmem(rows, f32), vmem(rows, f32), vmem(rows, f32),
            vmem(diag, f32), vmem(diag, f32), vmem(diag, f32), vmem(diag, f32),
            vmem(rows[1:], f32),
            vmem((2, rows_x, Z), f32), vmem((2, rows_x, Z), f32),
            vmem((2, Y, Z), f32), vmem((2, Y, Z), f32), vmem((2, 8, Z), f32),
            vmem((2, 8, Z), f32), vmem((2, 8, Z), f32),
            vmem((2 * SLOTS * SLOTS, LANES), f32), vmem((1, LANES), f32),
            vmem((devices, 1, LANES), f32), vmem((4, SLOTS, Z), f32),
            pltpu.SemaphoreType.DMA((6, STEPS)), pltpu.SemaphoreType.DMA((6, STEPS)),
            pltpu.SemaphoreType.DMA((devices,)), pltpu.SemaphoreType.DMA((devices,)),
            pltpu.SemaphoreType.DMA((2,)),
        ]
        out = pl.pallas_call(
            functools.partial(kernel, (gx_n, gy_n)),
            out_shape=(jax.ShapeDtypeStruct(field, f32),) * 2,
            in_specs=[pl.BlockSpec(memory_space=pl.ANY), pl.BlockSpec(memory_space=pl.ANY),
                      pl.BlockSpec(memory_space=pltpu.SMEM)],
            out_specs=(pl.BlockSpec(memory_space=vmem),) * 2,
            scratch_shapes=scratch,
            compiler_params=pltpu.CompilerParams(
                collective_id=0, has_side_effects=True, vmem_limit_bytes=48 * 1024 * 1024),
        )(source[0], permittivity, frequency)
        return out[0][None], out[1][None]

    placed = (P("groups", None, None, "gx", "gy", None), P("groups", "gx", "gy", None), P())
    return jax.shard_map(
        body,
        mesh=mesh,
        in_specs=placed,
        out_specs=(
            P("groups", None, None, "gx", "gy", None),
            P("groups", None, None, "gx", "gy", None),
        ),
        check_vma=False,
    )
```

time: 472 us -> 62.8 us (0.13)
  blocking collectives: 181 us -> 0 us
  between operations: 99.9 us -> 1.29 us
  other arithmetic: 74.5 us -> 0 us
  Pallas kernels: 0 us -> 57.4 us
  waiting for transfers between devices: 43.6 us -> 0 us
  starting transfers between devices: 38.4 us -> 0 us
  local copies, waits for them, and re-layouts: 31.8 us -> 3.88 us
    psum x6 -> x0, blocking collectives: 181 us -> none  [the longest x3 89.6 us: body(): lax.psum((product(second, middle), product(second, second), product(sourc...]
    pallas_call x0 -> x1, Pallas kernels: none -> 57.4 us  [body(): pl.pallas_call(functools.partial(kernel, (gx_n, gy_n)), out_shape=(jax.Sh...]
    ppermute x24 -> x0, waiting for transfers between devices: 43.6 us -> none  [shifted(): return lax.ppermute(array, axis, pairs)]
    sub x111 -> x0, other arithmetic: 41.9 us -> none  [the longest x15 27.3 us: scaled(): real_part = values[:, :, 0] * real_scale - values[:, :, 1] * imag_scale]
    ppermute x24 -> x0, starting transfers between devices: 38.4 us -> none  [shifted(): return lax.ppermute(array, axis, pairs)]
    another operation x36 -> x0, other arithmetic: 19.6 us -> none  [the longest x12 17.5 us: product(): return jnp.stack([real_part, imag_part])]
    slice x50 -> x0, local copies, waits for them, and re-layouts: 18.8 us -> none  [the longest x6 4.25 us: complex_ratio(): first[0] * other[0] + first[1] * other[1]]
    unnamed x173 -> x6, local copies, waits for them, and re-layouts: 12.9 us -> 3.88 us
  transfers between devices with their start and end apart: 24 -> 0, of which waited for: 17 -> 0; matrix products, arithmetic and copies ran while one was open for 2% -> 0% of each run, Pallas kernels for 0% -> 0%
where the time goes in v1:
time: 62.8 us; the launch traced here: 62.6 us
  Pallas kernels  57.4 us (91%)
  local copies, waits for them, and re-layouts  3.88 us (6%)
  between operations  1.29 us (2%)
    pallas_call x1, Pallas kernels, body(): pl.pallas_call(functools.partial(kernel, (gx_n, gy_n)), out_shape=(jax.Sh...  57.4 us
    unnamed x6, local copies, waits for them, and re-layouts  3.88 us

profile of v1, /device:TPU:0, one launch (start us, length us, event | category | flops | bytes accessed | tf_op | source)
XLA Modules:
  0.0 62.6 jit_solution(8011212257955776923)
XLA Ops:
  1.3 0.0 copy-start
  1.3 1.1 %copy-done = f32[1,3,2,4,32,256]{5,4,3,2,1,0:T(8,128)S(1)} copy-done((f32[1,3,2,4,32,256]{5,4,3,2,1,0:T(8,128)S(1)}, f32[1,3,2,4,32,256]{5,4,3,2,1,0:T(8,128)}, u32[]{:S(2)}) %copy-start) | copy-done | bytes 786456
  2.4 0.0 copy-start.1
  2.4 1.0 %copy-done.1 = f32[3,4,32,256]{3,2,1,0:T(8,128)S(1)} copy-done((f32[3,4,32,256]{3,2,1,0:T(8,128)S(1)}, f32[3,4,32,256]{3,2,1,0:T(8,128)}, u32[]{:S(2)}) %copy-start.1) | copy-done | bytes 393240
  3.4 57.4 %shard_map.50 = (f32[3,2,4,32,256]{4,3,2,1,0:T(8,128)S(1)}, f32[3,2,4,32,256]{4,3,2,1,0:T(8,128)S(1)}) custom-call(f32[3,2,4,32,256]{4,3,2,1,0:T(8,128)S(1)} %bitcast.5, f32[3,4,32,256]{3,2,1,0:T(8,128)S(1)} %copy-done.1, f32[1]{0:T(128)S(6)} %copy.7.freq), custom_call_target="tpu_custom_call" | custom-call | tf_op jit(solution)/shard_map/pallas_call | solution.py:500
  60.8 0.9 %copy.8 = f32[1,3,2,4,32,256]{5,4,3,2,1,0:T(8,128)} copy(f32[1,3,2,4,32,256]{5,4,3,2,1,0:T(8,128)S(1)} %bitcast.4) | data formatting | bytes 1572864
  61.7 0.9 %copy.9 = f32[1,3,2,4,32,256]{5,4,3,2,1,0:T(8,128)} copy(f32[1,3,2,4,32,256]{5,4,3,2,1,0:T(8,128)S(1)} %bitcast.3) | data formatting | bytes 1572864
Async XLA Ops:
  1.3 1.1 %copy-start = (f32[1,3,2,4,32,256]{5,4,3,2,1,0:T(8,128)S(1)}, f32[1,3,2,4,32,256]{5,4,3,2,1,0:T(8,128)}, u32[]{:S(2)}) copy-start(f32[1,3,2,4,32,256]{5,4,3,2,1,0:T(8,128)} %param.3) | copy-start | bytes 2359300
  2.4 1.0 %copy-start.1 = (f32[3,4,32,256]{3,2,1,0:T(8,128)S(1)}, f32[3,4,32,256]{3,2,1,0:T(8,128)}, u32[]{:S(2)}) copy-start(f32[3,4,32,256]{3,2,1,0:T(8,128)} %eps.1) | copy-start | bytes 1179652

commit v2 on v1

--- a/solution.py
+++ b/solution.py
@@ -193,12 +193,12 @@
 
     zero_row = jnp.zeros((1, Z), jnp.float32)
 
-    def dots(k):
+    def dots(k, layers, first=True):
         def one(j, carry):
             re = jnp.zeros((Y, Z), jnp.float32)
             im = jnp.zeros((Y, Z), jnp.float32)
             for component in range(3):
-                for x in range(X):
+                for x in layers:
                     a, b = cell(j, component, x), cell(k, component, x)
                     re = re + (a[0] * b[0] + a[1] * b[1])
                     im = im + (a[0] * b[1] - a[1] * b[0])
@@ -208,6 +208,9 @@
                 return sum(values[:, i:i + LANES] for i in range(0, Z, LANES))
 
             re, im = fold(re), fold(im)
+            if not first:
+                re = re + gram[pl.ds(j * SLOTS + k, 1)]
+                im = im + gram[pl.ds((SLOTS + j) * SLOTS + k, 1)]
             gram[pl.ds(j * SLOTS + k, 1)] = re
             gram[pl.ds(k * SLOTS + j, 1)] = re
             gram[pl.ds((SLOTS + j) * SLOTS + k, 1)] = im
@@ -254,33 +257,34 @@
                 value = a_k * (pair[part] - material * V[k, component, part, x])
                 V[k + 1, component, part, x] = value - b_k * V[before, component, part, x]
 
-    def step(k, carry):
-        a_k = jnp.where(k == 0, 1.0 / HALF, 2.0 / HALF).astype(jnp.float32)
-        b_k = jnp.where(k == 0, 0.0, 1.0).astype(jnp.float32)
-        top = X - 1
-
+    top = X - 1
+
+    def send_down(k):
         for part in range(2):
             send_dd[k, pl.ds(part, 1)] = V[k, 1, part, 0, pl.ds(Y - 1, 1)]
+        send(k, DIAG_DOWN)
+        send(k, DOWN)
+
+    def send_up(k):
+        for part in range(2):
             send_du[k, pl.ds(part, 1)] = V[k, 0, part, top, pl.ds(0, 1)]
-            for i, component in enumerate((0, 2)):
-                for x in range(X):
-                    send_yd[k, i, part, pl.ds(x, 1)] = V[k, component, part, x, pl.ds(0, 1)]
-        send(k, DIAG_DOWN)
         send(k, DIAG_UP)
-        send(k, Y_DOWN)
-        send(k, DOWN)
-
         ex, ey, ez = cell(k, 0, top), cell(k, 1, top), cell(k, 2, top)
         fx = row(fxt, X)
-        fy = whole(fyt)
         py_ = cadd(front_dz(ex), cmul(ez, fx))
-        dy = cmul(both(lambda a: next_y(a, zero_row) - a, ex), fy)
+        dy = cmul(both(lambda a: next_y(a, zero_row) - a, ex), whole(fyt))
         pz_ = cadd(cmul(ey, fx), dy)
         for part in range(2):
             send_p[k, 0, part] = py_[part]
             send_p[k, 1, part] = -pz_[part]
         send(k, UP)
 
+    def send_rows(k):
+        for part in range(2):
+            for i, component in enumerate((0, 2)):
+                for x in range(X):
+                    send_yd[k, i, part, pl.ds(x, 1)] = V[k, component, part, x, pl.ds(0, 1)]
+        send(k, Y_DOWN)
         fy = row(fyt, Y - 1)
         for x in range(X):
             at = pl.ds(Y - 1, 1)
@@ -296,6 +300,11 @@
                 send_yu[k, 1, part, pl.ds(x, 1)] = qz[part]
         send(k, Y_UP)
 
+    def step(k, down_first, last):
+        a_k = jnp.where(k == 0, 1.0 / HALF, 2.0 / HALF).astype(jnp.float32)
+        b_k = jnp.where(k == 0, 0.0, 1.0).astype(jnp.float32)
+        send_rows(k)
+
         receive(k, Y_DOWN)
         for x in range(X - 1):
             h_layer(k, x, cell(k, 1, x + 1), cell(k, 2, x + 1))
@@ -314,24 +323,44 @@
         for x in range(1, X - 1):
             out_layer(k, x, hcell(1, x - 1), hcell(2, x - 1), a_k, b_k)
 
-        dots(k)
-
-        receive(k, DIAG_DOWN)
-        fix = cmul((recv_dd[k, pl.ds(0, 1)], recv_dd[k, pl.ds(1, 1)]), row(fxt, X))
-        for part in range(2):
-            hrow[1, part, pl.ds(top, 1)] = hrow[1, part, pl.ds(top, 1)] + fix[part]
-        receive(k, DOWN)
-        h_layer(k, top, (recv_e[k, 0, 0], recv_e[k, 0, 1]), (recv_e[k, 1, 0], recv_e[k, 1, 1]))
-        out_layer(k, top, hcell(1, top - 1), hcell(2, top - 1), a_k, b_k)
-
-        receive(k, DIAG_UP)
-        receive(k, UP)
-        fx = row(fxt, 0)
-        hy = csub((recv_p[k, 0, 0], recv_p[k, 0, 1]), cmul(cell(k, 2, 0), fx))
-        hz = cadd((recv_p[k, 1, 0], recv_p[k, 1, 1]), cmul(cell(k, 1, 0), fx))
-        fix = cmul((recv_du[k, pl.ds(0, 1)], recv_du[k, pl.ds(1, 1)]), row(fyt, Y - 1))
-        hz = both(lambda a, f: jnp.where(iota((Y, Z), 0) == Y - 1, a - f, a), hz, fix)
-        out_layer(k, 0, hy, hz, a_k, b_k)
+        def from_above():
+            receive(k, DIAG_DOWN)
+            fix = cmul((recv_dd[k, pl.ds(0, 1)], recv_dd[k, pl.ds(1, 1)]), row(fxt, X))
+            for part in range(2):
+                hrow[1, part, pl.ds(top, 1)] = hrow[1, part, pl.ds(top, 1)] + fix[part]
+            receive(k, DOWN)
+            h_layer(k, top, (recv_e[k, 0, 0], recv_e[k, 0, 1]),
+                    (recv_e[k, 1, 0], recv_e[k, 1, 1]))
+            out_layer(k, top, hcell(1, top - 1), hcell(2, top - 1), a_k, b_k)
+            if not last:
+                send_up(k + 1)
+
+        def from_below():
+            receive(k, DIAG_UP)
+            receive(k, UP)
+            fx = row(fxt, 0)
+            hy = csub((recv_p[k, 0, 0], recv_p[k, 0, 1]), cmul(cell(k, 2, 0), fx))
+            hz = cadd((recv_p[k, 1, 0], recv_p[k, 1, 1]), cmul(cell(k, 1, 0), fx))
+            fix = cmul((recv_du[k, pl.ds(0, 1)], recv_du[k, pl.ds(1, 1)]), row(fyt, Y - 1))
+            hz = both(lambda a, f: jnp.where(iota((Y, Z), 0) == Y - 1, a - f, a), hz, fix)
+            out_layer(k, 0, hy, hz, a_k, b_k)
+            if not last:
+                send_down(k + 1)
+
+        halves = [from_above, from_below]
+        if not down_first:
+            halves.reverse()
+        dots(k, range(X))
+        if last:
+            dots(k + 1, range(1, X - 1))
+        halves[0]()
+        halves[1]()
+        if last:
+            dots(k + 1, sorted({0, top}), first=X < 3)
+
+    def two_steps(pair, carry):
+        step(2 * pair, True, False)
+        step(2 * pair + 1, True, False)
         return carry
 
     load_eps.wait()
@@ -342,8 +371,11 @@
     load_src.wait()
     pl.semaphore_wait(barrier, devices - 1)
 
-    lax.fori_loop(0, STEPS, step, 0)
-    dots(STEPS)
+    send_down(0)
+    send_up(0)
+    lax.fori_loop(0, STEPS // 2 - 1, two_steps, 0)
+    step(jnp.int32(STEPS - 2), True, False)
+    step(jnp.int32(STEPS - 1), True, True)
 
     sums = jnp.sum(gram[...], axis=1, keepdims=True)
     count = 2 * SLOTS * SLOTS
@@ -439,21 +471,24 @@
         for at in range(0, Z, LANES):
             coef[i, :, pl.ds(at, LANES)] = values
 
+    chunk = 16 if Y % 16 == 0 else 8
+
     def emit(index, carry):
-        component = index // X
-        x = lax.rem(index, X)
-        for out, base, last in ((x_out, 0, STEPS), (r_out, 2, STEPS + 1)):
-            re = im = jnp.zeros((Y, Z), jnp.float32)
-            for k in range(last):
-                c = coef[base, pl.ds(k, 1)], coef[base + 1, pl.ds(k, 1)]
-                v = V[k, component, 0, x], V[k, component, 1, x]
-                p = cmul(v, c)
-                re, im = re + p[0], im + p[1]
-            out[component, 0, x] = re
-            out[component, 1, x] = im
-        return carry
-
-    lax.fori_loop(0, 3 * X, emit, 0)
+        at = pl.ds(pl.multiple_of(lax.rem(index, Y // chunk) * chunk, 8), chunk)
+        index = index // (Y // chunk)
+        component, x = index // X, lax.rem(index, X)
+        sums = [jnp.zeros((chunk, Z), jnp.float32)] * 4
+        for k in range(STEPS + 1):
+            v = V[k, component, 0, x, at], V[k, component, 1, x, at]
+            for base in ((0, 2) if k < STEPS else (2,)):
+                p = cmul(v, (coef[base, pl.ds(k, 1)], coef[base + 1, pl.ds(k, 1)]))
+                sums[base], sums[base + 1] = sums[base] + p[0], sums[base + 1] + p[1]
+        for part in range(2):
+            x_out[component, part, x, at] = sums[part]
+            r_out[component, part, x, at] = sums[2 + part]
+        return carry
+
+    lax.fori_loop(0, 3 * X * (Y // chunk), emit, 0)
 
     def drain(k, carry):
         for message, sends, _ in messages(k).values():
@@ -500,7 +535,7 @@
         out = pl.pallas_call(
             functools.partial(kernel, (gx_n, gy_n)),
             out_shape=(jax.ShapeDtypeStruct(field, f32),) * 2,
-            in_specs=[pl.BlockSpec(memory_space=pl.ANY), pl.BlockSpec(memory_space=pl.ANY),
+            in_specs=[pl.BlockSpec(memory_space=pltpu.HBM), pl.BlockSpec(memory_space=pltpu.HBM),
                       pl.BlockSpec(memory_space=pltpu.SMEM)],
             out_specs=(pl.BlockSpec(memory_space=vmem),) * 2,
             scratch_shapes=scratch,

time: 62.8 us -> 61 us (0.971)
  Pallas kernels: 57.4 us -> 55.6 us
    pallas_call x1, Pallas kernels: 57.4 us -> 55.6 us  [body(): pl.pallas_call(functools.partial(kernel, (gx_n, gy_n)), out_shape=(jax.Sh...]
where the time goes in v2:
time: 61 us; the launch traced here: 60.8 us
  Pallas kernels  55.6 us (91%)
  local copies, waits for them, and re-layouts  3.88 us (6%)
  between operations  1.29 us (2%)
    pallas_call x1, Pallas kernels, body(): pl.pallas_call(functools.partial(kernel, (gx_n, gy_n)), out_shape=(jax.Sh...  55.6 us
    unnamed x6, local copies, waits for them, and re-layouts  3.88 us

profile of v2, /device:TPU:0, one launch (start us, length us, event | category | flops | bytes accessed | tf_op | source)
XLA Modules:
  0.0 60.8 jit_solution(12767786364300980683)
XLA Ops:
  1.3 0.0 copy-start
  1.3 1.1 %copy-done = f32[1,3,2,4,32,256]{5,4,3,2,1,0:T(8,128)S(1)} copy-done((f32[1,3,2,4,32,256]{5,4,3,2,1,0:T(8,128)S(1)}, f32[1,3,2,4,32,256]{5,4,3,2,1,0:T(8,128)}, u32[]{:S(2)}) %copy-start) | copy-done | bytes 786456
  2.4 0.0 copy-start.1
  2.4 1.0 %copy-done.1 = f32[3,4,32,256]{3,2,1,0:T(8,128)S(1)} copy-done((f32[3,4,32,256]{3,2,1,0:T(8,128)S(1)}, f32[3,4,32,256]{3,2,1,0:T(8,128)}, u32[]{:S(2)}) %copy-start.1) | copy-done | bytes 393240
  3.4 55.6 %shard_map.50 = (f32[3,2,4,32,256]{4,3,2,1,0:T(8,128)S(1)}, f32[3,2,4,32,256]{4,3,2,1,0:T(8,128)S(1)}) custom-call(f32[3,2,4,32,256]{4,3,2,1,0:T(8,128)S(1)} %bitcast.5, f32[3,4,32,256]{3,2,1,0:T(8,128)S(1)} %copy-done.1, f32[1]{0:T(128)S(6)} %copy.7.freq), custom_call_target="tpu_custom_call" | custom-call | tf_op jit(solution)/shard_map/pallas_call | solution.py:535
  59.0 0.9 %copy.8 = f32[1,3,2,4,32,256]{5,4,3,2,1,0:T(8,128)} copy(f32[1,3,2,4,32,256]{5,4,3,2,1,0:T(8,128)S(1)} %bitcast.4) | data formatting | bytes 1572864
  59.9 0.9 %copy.9 = f32[1,3,2,4,32,256]{5,4,3,2,1,0:T(8,128)} copy(f32[1,3,2,4,32,256]{5,4,3,2,1,0:T(8,128)S(1)} %bitcast.3) | data formatting | bytes 1572864
Async XLA Ops:
  1.3 1.1 %copy-start = (f32[1,3,2,4,32,256]{5,4,3,2,1,0:T(8,128)S(1)}, f32[1,3,2,4,32,256]{5,4,3,2,1,0:T(8,128)}, u32[]{:S(2)}) copy-start(f32[1,3,2,4,32,256]{5,4,3,2,1,0:T(8,128)} %param.3) | copy-start | bytes 2359300
  2.4 1.0 %copy-start.1 = (f32[3,4,32,256]{3,2,1,0:T(8,128)S(1)}, f32[3,4,32,256]{3,2,1,0:T(8,128)}, u32[]{:S(2)}) copy-start(f32[3,4,32,256]{3,2,1,0:T(8,128)} %eps.1) | copy-start | bytes 1179652

commit v3 on v2

--- a/solution.py
+++ b/solution.py
@@ -541,7 +541,7 @@
             scratch_shapes=scratch,
             compiler_params=pltpu.CompilerParams(
                 collective_id=0, has_side_effects=True, vmem_limit_bytes=48 * 1024 * 1024),
-        )(source[0], permittivity, frequency)
+        )(pltpu.with_memory_space_constraint(source[0], pltpu.HBM), pltpu.with_memory_space_constraint(permittivity, pltpu.HBM), frequency)
         return out[0][None], out[1][None]
 
     placed = (P("groups", None, None, "gx", "gy", None), P("groups", "gx", "gy", None), P())

time: 61 us -> 59.9 us (0.982)
  local copies, waits for them, and re-layouts: 3.88 us -> 1.76 us
  Pallas kernels: 55.6 us -> 56.7 us
    unnamed x6 -> x2, local copies, waits for them, and re-layouts: 3.88 us -> 1.76 us
    pallas_call x1, Pallas kernels: 55.6 us -> 56.7 us  [body(): pl.pallas_call(functools.partial(kernel, (gx_n, gy_n)), out_shape=(jax.Sh...]
where the time goes in v3:
time: 59.9 us; the launch traced here: 59.7 us
  Pallas kernels  56.7 us (95%)
  local copies, waits for them, and re-layouts  1.76 us (3%)
  between operations  1.28 us (2%)
    pallas_call x1, Pallas kernels, body(): pl.pallas_call(functools.partial(kernel, (gx_n, gy_n)), out_shape=(jax.Sh...  56.7 us
    unnamed x2, local copies, waits for them, and re-layouts  1.76 us

profile of v3, /device:TPU:0, one launch (start us, length us, event | category | flops | bytes accessed | tf_op | source)
XLA Modules:
  0.0 59.7 jit_solution(16967686588140377207)
XLA Ops:
  1.3 56.7 %shard_map.50 = (f32[3,2,4,32,256]{4,3,2,1,0:T(8,128)S(1)}, f32[3,2,4,32,256]{4,3,2,1,0:T(8,128)S(1)}) custom-call(f32[3,2,4,32,256]{4,3,2,1,0:T(8,128)} %bitcast.5, f32[3,4,32,256]{3,2,1,0:T(8,128)} %eps.1, f32[1]{0:T(128)S(6)} %copy.7.freq), custom_call_target="tpu_custom_call" | custom-call | tf_op jit(solution)/shard_map/pallas_call | solution.py:535
  58.0 0.9 %copy.8 = f32[1,3,2,4,32,256]{5,4,3,2,1,0:T(8,128)} copy(f32[1,3,2,4,32,256]{5,4,3,2,1,0:T(8,128)S(1)} %bitcast.4) | data formatting | bytes 1572864
  58.8 0.9 %copy.9 = f32[1,3,2,4,32,256]{5,4,3,2,1,0:T(8,128)} copy(f32[1,3,2,4,32,256]{5,4,3,2,1,0:T(8,128)S(1)} %bitcast.3) | data formatting | bytes 1572864
